TPU v7x, 32 devices: a whole 2x2x4 slice. The times are simulated.
32 devices in a mesh: groups: 2 (over y), beam: 8 (over z, x), mp: 2 (over core).
Axes of the slice: x: 2, y: 2, z: 4, core: 2. Of those that a mesh axis runs over, the one named last changes fastest.
Arguments:
- states: float32 [64, 8, 128, 128], P(('groups', 'beam'), 'mp'), parts along dimension 0, may hold values from -4 to 4
- parent_beam: int32 [64], P(('groups', 'beam')), parts along dimension 0, may hold values from 0 to 7, as said below
- next_token: int32 [64], P(('groups', 'beam')), parts along dimension 0, may hold values from 0 to 1023
- proj_table: bfloat16 [1024, 8, 640], P('beam', 'mp'), may hold values from -6 to 6
- gate_table: bfloat16 [1024, 3, 8], P('beam', None, 'mp'), may hold values from -6 to 6
- gain: float32 [8, 128], P('mp'), may hold values from 0.1 to 1.9
Outputs:
- readout: bfloat16 [64, 8, 128], P(('groups', 'beam'), 'mp'), parts along dimension 0
- new_states: float32 [64, 8, 128, 128], P(('groups', 'beam'), 'mp'), parts along dimension 0
There are 2 independent parts, one for each index of `groups`. A program takes and returns all parts, laid end to end along the dimension named above; an argument that names none is the same for every part. Nothing has to cross between parts.
Inputs may be any that keep to these rules, and one draw needn't show every extreme that they name: The parent of hypothesis h = b * 4 + u is parent_beam[h] * 4 + u. In each aligned block of 4 hypotheses at most 2 take their parent from any one beam other than their own beam, and every block has a beam that supplies exactly 2.
All inputs are finite; a program needn't handle non-finite values.
Results may differ from a plain program's by a relative error of at most 0.001.
Values may be sent and summed in bfloat16 or wider, within the bound.
A program may use at most 64 MiB of HBM per device.

v0:
```python
import jax
import jax.numpy as jnp
from jax import lax
from jax.sharding import PartitionSpec as P

HEAD_DIM = 128
BEAMS = 8
CAP = 2


def from_behind(block, axis, distance):
    devices = range(lax.axis_size(axis))
    route = [((i - distance) % len(devices), i) for i in devices]
    return lax.ppermute(block, axis, route)


def unit_norm(vector):
    return vector * lax.rsqrt(jnp.sum(vector * vector, axis=-1, keepdims=True) + 1e-06)


def advance(parents, entries, gate_entries, gain):
    retain = jax.nn.sigmoid(gate_entries[:, 0, :])
    strengths = 2.0 * jax.nn.sigmoid(gate_entries[:, 1:, :])
    state_now = retain[:, :, None, None] * parents
    for reflect in range(2):
        key_unit = unit_norm(entries[:, :, 1 + reflect, :])
        value_row = entries[:, :, 3 + reflect, :]
        applied = jnp.einsum("nhvd,nhd->nhv", state_now, key_unit, precision=lax.Precision.HIGHEST)
        state_now = (
            state_now
            - strengths[:, reflect, :, None, None]
            * (applied - value_row)[:, :, :, None]
            * key_unit[:, :, None, :]
        )
    query_unit = unit_norm(entries[:, :, 0, :])
    readout = jnp.einsum("nhvd,nhd->nhv", state_now, query_unit, precision=lax.Precision.HIGHEST)
    normed = (
        gain[None, :, :]
        * readout
        * lax.rsqrt(jnp.mean(readout * readout, axis=-1, keepdims=True) + 1e-05)
    )
    return (normed.astype(jnp.bfloat16), state_now)


def local(states, parent_beam, next_token, proj_table, gate_table, gain):
    hyp_rows = states.shape[0]
    head_count = states.shape[1]
    devices = lax.axis_size("beam")
    spacing = devices // BEAMS
    position = lax.axis_index("beam")
    my_beam = position // spacing
    offset = (my_beam - parent_beam) % BEAMS
    tokens_all, parents_all = (
        lax.all_gather(next_token, "beam", axis=0, tiled=True),
        lax.all_gather(parent_beam, "beam", axis=0, tiled=True),
    )
    vocab_rows = proj_table.shape[0]
    local_ids = tokens_all - position * vocab_rows
    onehot = (local_ids[:, None] == jnp.arange(vocab_rows, dtype=jnp.int32)[None, :]).astype(
        jnp.bfloat16
    )
    flat_table = proj_table.reshape(vocab_rows, head_count * 5 * HEAD_DIM)
    flat_gates = gate_table.reshape(vocab_rows, 3 * head_count)
    looked = jnp.dot(onehot, flat_table, preferred_element_type=jnp.float32).astype(jnp.bfloat16)
    looked_gates = jnp.dot(onehot, flat_gates, preferred_element_type=jnp.float32).astype(
        jnp.bfloat16
    )
    looked = looked.reshape(devices, hyp_rows, head_count * 5 * HEAD_DIM)
    looked_gates = looked_gates.reshape(devices, hyp_rows, 3 * head_count)
    arrived, arrived_gates = (
        lax.all_to_all(looked, "beam", split_axis=0, concat_axis=0, tiled=True),
        lax.all_to_all(looked_gates, "beam", split_axis=0, concat_axis=0, tiled=True),
    )
    entries = jnp.sum(arrived, axis=0, dtype=jnp.float32).reshape(hyp_rows, head_count, 5, HEAD_DIM)
    gate_entries = jnp.sum(arrived_gates, axis=0, dtype=jnp.float32).reshape(
        hyp_rows, 3, head_count
    )
    parents = jnp.where((offset == 0)[:, None, None, None], states, jnp.zeros_like(states))
    slot_ids = jnp.arange(CAP, dtype=jnp.int32)
    for distance in range(1, BEAMS):
        target = (position + distance * spacing) % devices
        their_parents = lax.dynamic_slice_in_dim(parents_all, target * hyp_rows, hyp_rows)
        needed = their_parents == my_beam
        slot_rank = jnp.cumsum(needed.astype(jnp.int32)) - 1
        select = ((slot_rank[None, :] == slot_ids[:, None]) & needed[None, :]).astype(jnp.float32)
        packed = jnp.einsum("cr,rhij->chij", select, states, precision=lax.Precision.HIGHEST)
        received = from_behind(packed, "beam", distance * spacing)
        wanted = offset == distance
        wanted_rank = jnp.cumsum(wanted.astype(jnp.int32)) - 1
        placing = ((wanted_rank[:, None] == slot_ids[None, :]) & wanted[:, None]).astype(
            jnp.float32
        )
        parents = parents + jnp.einsum(
            "rc,chij->rhij", placing, received, precision=lax.Precision.HIGHEST
        )
    return advance(parents, entries, gate_entries, gain)


def solution(mesh):
    return jax.shard_map(
        local,
        mesh=mesh,
        in_specs=(
            P(("groups", "beam"), "mp", None, None),
            P(("groups", "beam")),
            P(("groups", "beam")),
            P("beam", "mp", None),
            P("beam", None, "mp"),
            P("mp", None),
        ),
        out_specs=(P(("groups", "beam"), "mp", None), P(("groups", "beam"), "mp", None, None)),
        check_vma=False,
    )
```

profile of v0, /device:TPU:0, one launch (start us, length us, event | category | flops | bytes accessed | tf_op | source)
XLA Modules:
  0.0 151.5 jit_solution(17628549391322259586)
XLA Ops:
  4.2 13.1 %all-reduce.2 = (s32[32]{0:T(128)S(1)}, s32[32]{0:T(128)S(1)}) all-reduce(s32[32]{0:T(128)S(1)} %dynamic-update-slice.1, s32[32]{0:T(128)S(1)} %dynamic-update-slice), channel_id=1, replica_groups=mesh['groups'=2,'beam'=8,'mp'=2] {'beam'}, use_global_device_ids=true, to_apply=%add.1 | all-reduce | flops 64 | bytes 512
  17.6 3.7 %fusion.13 = f32[2,4,128,128]{3,0,2,1:T(2,128)} fusion(f32[4,4,128,128]{3,2,1,0:T(8,128)} %param.6, pred[4]{0:T(512)(128)(4,1)S(1)} %get-tuple-element.56, s32[4]{0:T(128)S(1)} %add_bitcast_fusion.2), kind=kOutput, calls=%fused_computation.19 | convolution fusion | flops 6291472 | bytes 1572884 | tf_op jit(solution)/shard_map/cr,rhij->chij/dot_general | solution.py:86
  21.5 2.5 %fusion.15 = f32[2,4,128,128]{3,0,2,1:T(2,128)} fusion(f32[4,4,128,128]{3,2,1,0:T(8,128)S(1)} %copy-done, pred[4]{0:T(512)(128)(4,1)S(1)} %get-tuple-element.54, s32[4]{0:T(128)S(1)} %add_bitcast_fusion.4), kind=kOutput, calls=%fused_computation.21 | convolution fusion | flops 6291472 | bytes 1572884 | tf_op jit(solution)/shard_map/cr,rhij->chij/dot_general | solution.py:86
  23.9 2.8 %collective-permute-start.4 = (f32[2,4,128,128]{3,0,2,1:T(2,128)}, f32[2,4,128,128]{3,0,2,1:T(2,128)S(1)}, u32[]{:S(2)}, u32[]{:S(2)}) collective-permute-start(f32[2,4,128,128]{3,0,2,1:T(2,128)} %fusion.15), channel_id=1, source_target_pairs={{6,0},{8,2},{10,4},{12,6},{14,8},{0,10},{2,12},{4,14},{7,1},{9,3},... | collective-permute-start | bytes 1572872 | tf_op jit(solution)/shard_map/ppermute | solution.py:14
  27.0 1.7 %fusion.17 = f32[2,4,128,128]{3,0,2,1:T(2,128)S(1)} fusion(f32[4,4,128,128]{3,2,1,0:T(8,128)S(1)} %copy-done, pred[4]{0:T(512)(128)(4,1)S(1)} %get-tuple-element.52, s32[4]{0:T(128)S(1)} %add_bitcast_fusion.6), kind=kOutput, calls=%fused_computation.23 | convolution fusion | flops 6291472 | bytes 1572884 | tf_op jit(solution)/shard_map/cr,rhij->chij/dot_general | solution.py:86
  30.1 2.5 %fusion.19 = f32[2,4,128,128]{3,0,2,1:T(2,128)} fusion(f32[4,4,128,128]{3,2,1,0:T(8,128)S(1)} %copy-done, pred[4]{0:T(512)(128)(4,1)S(1)} %get-tuple-element.50, s32[4]{0:T(128)S(1)} %add_bitcast_fusion.8), kind=kOutput, calls=%fused_computation.25 | convolution fusion | flops 6291472 | bytes 1572884 | tf_op jit(solution)/shard_map/cr,rhij->chij/dot_general | solution.py:86
  33.5 2.5 %fusion.21 = f32[2,4,128,128]{3,0,2,1:T(2,128)} fusion(f32[4,4,128,128]{3,2,1,0:T(8,128)S(1)} %copy-done, pred[4]{0:T(512)(128)(4,1)S(1)} %get-tuple-element.48, s32[4]{0:T(128)S(1)} %add_bitcast_fusion.10), kind=kOutput, calls=%fused_computation.27 | convolution fusion | flops 6291472 | bytes 1572884 | tf_op jit(solution)/shard_map/cr,rhij->chij/dot_general | solution.py:86
  36.0 1.4 collective-permute-start.1
  38.3 5.7 %all-to-all-start = ((bf16[8,4,12]{2,1,0:T(4,128)(2,1)}), bf16[8,4,12]{2,1,0:T(4,128)(2,1)S(1)}, u32[]{:S(2)}, u32[]{:S(2)}) async-start(bf16[8,4,12]{2,1,0:T(4,128)(2,1)} %bitcast.1), calls=%async_computation | async-start | bytes 16384 | tf_op jit(solution)/shard_map/all_to_all | solution.py:72
  45.8 1.7 %fusion.23 = f32[2,4,128,128]{3,0,2,1:T(2,128)S(1)} fusion(f32[4,4,128,128]{3,2,1,0:T(8,128)S(1)} %copy-done, pred[4]{0:T(512)(128)(4,1)S(1)} %get-tuple-element.11, s32[4]{0:T(128)S(1)} %add_bitcast_fusion.12), kind=kOutput, calls=%fused_computation.29 | convolution fusion | flops 6291472 | bytes 1572884 | tf_op jit(solution)/shard_map/cr,rhij->chij/dot_general | solution.py:86
  47.5 2.5 %fusion.11 = f32[2,4,128,128]{3,0,2,1:T(2,128)} fusion(f32[4,4,128,128]{3,2,1,0:T(8,128)S(1)} %copy-done, pred[4]{0:T(512)(128)(4,1)S(1)} %get-tuple-element.58, s32[4]{0:T(128)S(1)} %add_bitcast_fusion), kind=kOutput, calls=%fused_computation.17 | convolution fusion | flops 6291472 | bytes 1572884 | tf_op jit(solution)/shard_map/cr,rhij->chij/dot_general | solution.py:86
  50.8 50.1 %all-to-all-done = bf16[8,4,12]{2,1,0:T(4,128)(2,1)S(1)} async-done(((bf16[8,4,12]{2,1,0:T(4,128)(2,1)}), bf16[8,4,12]{2,1,0:T(4,128)(2,1)S(1)}, u32[]{:S(2)}, u32[]{:S(2)}) %all-to-all-start) | async-done | bytes 800 | tf_op jit(solution)/shard_map/all_to_all | solution.py:72
  101.0 3.4 %all-to-all-start.1 = ((bf16[8,4,2560]{2,1,0:T(4,128)(2,1)}), bf16[8,4,2560]{2,1,0:T(4,128)(2,1)S(1)}, u32[]{:S(2)}, u32[]{:S(2)}) async-start(bf16[8,4,2560]{2,1,0:T(4,128)(2,1)} %reshape.478), calls=%async_computation.1 | async-start | bytes 327680 | tf_op jit(solution)/shard_map/all_to_all | solution.py:71
  104.6 7.3 %all-to-all-done.1 = bf16[8,4,2560]{2,1,0:T(4,128)(2,1)S(1)} async-done(((bf16[8,4,2560]{2,1,0:T(4,128)(2,1)}), bf16[8,4,2560]{2,1,0:T(4,128)(2,1)S(1)}, u32[]{:S(2)}, u32[]{:S(2)}) %all-to-all-start.1) | async-done | bytes 163872 | tf_op jit(solution)/shard_map/all_to_all | solution.py:71
  115.0 4.1 %collective-permute-start.6 = (f32[2,4,128,128]{3,0,2,1:T(2,128)S(1)}, f32[2,4,128,128]{3,0,2,1:T(2,128)S(1)}, u32[]{:S(2)}, u32[]{:S(2)}) collective-permute-start(f32[2,4,128,128]{3,0,2,1:T(2,128)S(1)} %copy-done.3), channel_id=1, source_target_pairs={{2,0},{4,2},{6,4},{8,6},{10,8},{12,10},{14,12},{0,14},{3,1},{5,3},... | collective-permute-start | bytes 1572872 | tf_op jit(solution)/shard_map/ppermute | solution.py:14
  120.3 2.3 %fusion.44 = f32[4,4,128,128]{3,0,2,1:T(4,128)S(1)} fusion(f32[2,4,128,128]{3,0,2,1:T(2,128)} %collective-permute-done.3, pred[4]{0:T(512)(128)(4,1)S(1)} %get-tuple-element.43, s32[4]{0:T(128)S(1)} %add_bitcast_fusion.7), kind=kOutput, calls=%fused_computation.72 | convolution fusion | flops 6291472 | bytes 1572884 | tf_op jit(solution)/shard_map/rc,chij->rhij/dot_general | solution.py:93
  122.7 2.3 %fusion.47 = f32[4,4,128,128]{3,0,2,1:T(4,128)S(1)} fusion(f32[2,4,128,128]{3,0,2,1:T(2,128)} %collective-permute-done.2, pred[4]{0:T(512)(128)(4,1)S(1)} %get-tuple-element.44, s32[4]{0:T(128)S(1)} %add_bitcast_fusion.9), kind=kOutput, calls=%fused_computation.75 | convolution fusion | flops 6291472 | bytes 1572884 | tf_op jit(solution)/shard_map/rc,chij->rhij/dot_general | solution.py:93
  125.1 2.3 %fusion.50 = f32[4,4,128,128]{3,0,2,1:T(4,128)S(1)} fusion(f32[2,4,128,128]{3,0,2,1:T(2,128)} %collective-permute-done.1, pred[4]{0:T(512)(128)(4,1)S(1)} %get-tuple-element.45, s32[4]{0:T(128)S(1)} %add_bitcast_fusion.11), kind=kOutput, calls=%fused_computation.78 | convolution fusion | flops 6291472 | bytes 1572884 | tf_op jit(solution)/shard_map/rc,chij->rhij/dot_general | solution.py:93
  127.4 10.4 %collective-permute-done.6 = f32[2,4,128,128]{3,0,2,1:T(2,128)S(1)} collective-permute-done((f32[2,4,128,128]{3,0,2,1:T(2,128)S(1)}, f32[2,4,128,128]{3,0,2,1:T(2,128)S(1)}, u32[]{:S(2)}, u32[]{:S(2)}) %collective-permute-start.6) | collective-permute-done | bytes 524320 | tf_op jit(solution)/shard_map/ppermute | solution.py:14
  139.2 2.7 %fusion.6 = f32[4,4,128,128]{3,0,2,1:T(4,128)S(1)} fusion(f32[4,4,128,128]{3,0,2,1:T(4,128)S(1)} %fusion.35, f32[4,4,128,128]{3,0,2,1:T(4,128)S(1)} %fusion.38, f32[4,4,128,128]{3,0,2,1:T(4,128)S(1)} %fusion.41, f32[4,4,128,128]{3,0,2,1:T(4,128)S(1)} %fusion.44, f32[4,4,128,128]{3,0,2,1:T(4,128)S(1)} %fusion.47, f32[4,4,128,128]{3,0,2,1:T(4,128)S(1)} %fusion.50, ...), kind=kOutput, calls=%fused_computation.8 | convolution fusion | flops 8650768 | bytes 8912984 | tf_op jit(solution)/shard_map/rc,chij->rhij/dot_general | solution.py:93
  141.9 1.7 %fusion.9 = f32[4,4,1,128]{3,2,1,0:T(1,128)S(1)} fusion(f32[4,4,128,1]{2,3,1,0:T(1,128)S(1)} %bitcast.181, f32[4,4,128,128]{3,0,2,1:T(4,128)S(1)} %fusion.6), kind=kOutput, calls=%fused_computation.12 | convolution fusion | flops 3145728 | bytes 1064960 | tf_op jit(solution)/shard_map/nhvd,nhd->nhv/dot_general | solution.py:28
  144.9 1.7 %fusion.7 = f32[4,4,1,128]{3,2,1,0:T(1,128)S(1)} fusion(f32[4,4,128,1]{2,3,1,0:T(1,128)S(1)} %bitcast.182, f32[4,4,128,128]{3,0,2,1:T(4,128)S(1)} %multiply_subtract_fusion.1), kind=kOutput, calls=%fused_computation.10 | convolution fusion | flops 3145728 | bytes 1064960 | tf_op jit(solution)/shard_map/nhvd,nhd->nhv/dot_general | solution.py:28
  146.8 1.4 multiply_subtract_fusion
  148.3 1.7 %fusion.128 = f32[4,4,1,128]{3,2,1,0:T(1,128)S(1)} fusion(f32[4,4,128,128]{3,2,1,0:T(8,128)S(1)} %copy.22, f32[4,4,128,1]{2,3,1,0:T(1,128)S(1)} %bitcast.180), kind=kOutput, calls=%fused_computation.201 | convolution fusion | flops 3145728 | bytes 1064960 | tf_op jit(solution)/shard_map/nhvd,nhd->nhv/dot_general | solution.py:36
  (101 shorter events, 18.3 us)
Async XLA Ops:
  0.6 0.7 copy-start.7
  0.6 20.8 %copy-start = (f32[4,4,128,128]{3,2,1,0:T(8,128)S(1)}, f32[4,4,128,128]{3,2,1,0:T(8,128)}, u32[]{:S(2)}) copy-start(f32[4,4,128,128]{3,2,1,0:T(8,128)} %param.6) | copy-start | bytes 3145732
  21.3 91.4 %collective-permute-start.5 = (f32[2,4,128,128]{3,0,2,1:T(2,128)}, f32[2,4,128,128]{3,0,2,1:T(2,128)S(1)}, u32[]{:S(2)}, u32[]{:S(2)}) collective-permute-start(f32[2,4,128,128]{3,0,2,1:T(2,128)} %fusion.13), channel_id=1, source_target_pairs={{4,0},{6,2},{8,4},{10,6},{12,8},{14,10},{0,12},{2,14},{5,1},{7,3},... | collective-permute-start | bytes 1572872 | tf_op jit(solution)/shard_map/ppermute | solution.py:14
  23.9 91.0 %collective-permute-start.4 = (f32[2,4,128,128]{3,0,2,1:T(2,128)}, f32[2,4,128,128]{3,0,2,1:T(2,128)S(1)}, u32[]{:S(2)}, u32[]{:S(2)}) collective-permute-start(f32[2,4,128,128]{3,0,2,1:T(2,128)} %fusion.15), channel_id=1, source_target_pairs={{6,0},{8,2},{10,4},{12,6},{14,8},{0,10},{2,12},{4,14},{7,1},{9,3},... | collective-permute-start | bytes 1572872 | tf_op jit(solution)/shard_map/ppermute | solution.py:14
  28.6 91.7 %collective-permute-start.3 = (f32[2,4,128,128]{3,0,2,1:T(2,128)S(1)}, f32[2,4,128,128]{3,0,2,1:T(2,128)}, u32[]{:S(2)}, u32[]{:S(2)}) collective-permute-start(f32[2,4,128,128]{3,0,2,1:T(2,128)S(1)} %fusion.17), channel_id=1, source_target_pairs={{8,0},{10,2},{12,4},{14,6},{0,8},{2,10},{4,12},{6,14},{9,1},{11,3}... | collective-permute-start | bytes 1572872 | tf_op jit(solution)/shard_map/ppermute | solution.py:14
  32.6 90.1 %collective-permute-start.2 = (f32[2,4,128,128]{3,0,2,1:T(2,128)}, f32[2,4,128,128]{3,0,2,1:T(2,128)}, u32[]{:S(2)}, u32[]{:S(2)}) collective-permute-start(f32[2,4,128,128]{3,0,2,1:T(2,128)} %fusion.19), channel_id=1, source_target_pairs={{10,0},{12,2},{14,4},{0,6},{2,8},{4,10},{6,12},{8,14},{11,1},{13,3... | collective-permute-start | bytes 1572872 | tf_op jit(solution)/shard_map/ppermute | solution.py:14
  33.5 3.8 %copy-start.4 = (bf16[128,3,4]{0,2,1:T(4,128)(2,1)S(1)}, bf16[128,3,4]{0,2,1:T(4,128)(2,1)}, u32[]{:S(2)}) copy-start(bf16[128,3,4]{0,2,1:T(4,128)(2,1)} %param.10) | copy-start | bytes 9220
  33.5 12.0 %copy-start.2 = (bf16[128,4,640]{2,1,0:T(4,128)(2,1)S(1)}, bf16[128,4,640]{2,1,0:T(4,128)(2,1)}, u32[]{:S(2)}) copy-start(bf16[128,4,640]{2,1,0:T(4,128)(2,1)} %param.9) | copy-start | bytes 1966084
  36.0 89.1 %collective-permute-start.1 = (f32[2,4,128,128]{3,0,2,1:T(2,128)}, f32[2,4,128,128]{3,0,2,1:T(2,128)}, u32[]{:S(2)}, u32[]{:S(2)}) collective-permute-start(f32[2,4,128,128]{3,0,2,1:T(2,128)} %fusion.21), channel_id=1, source_target_pairs={{12,0},{14,2},{0,4},{2,6},{4,8},{6,10},{8,12},{10,14},{13,1},{15,3... | collective-permute-start | bytes 1572872 | tf_op jit(solution)/shard_map/ppermute | solution.py:14
  38.3 5.7 %copy-start.6 = (s32[4]{0:T(128)S(1)}, s32[4]{0:T(128)}, u32[]{:S(2)}) copy-start(s32[4]{0:T(128)} %param.7) | copy-start | bytes 52
  38.3 62.7 %all-to-all-start = ((bf16[8,4,12]{2,1,0:T(4,128)(2,1)}), bf16[8,4,12]{2,1,0:T(4,128)(2,1)S(1)}, u32[]{:S(2)}, u32[]{:S(2)}) async-start(bf16[8,4,12]{2,1,0:T(4,128)(2,1)} %bitcast.1), calls=%async_computation | async-start | bytes 16384 | tf_op jit(solution)/shard_map/all_to_all | solution.py:72
  101.0 11.0 %all-to-all-start.1 = ((bf16[8,4,2560]{2,1,0:T(4,128)(2,1)}), bf16[8,4,2560]{2,1,0:T(4,128)(2,1)S(1)}, u32[]{:S(2)}, u32[]{:S(2)}) async-start(bf16[8,4,2560]{2,1,0:T(4,128)(2,1)} %reshape.478), calls=%async_computation.1 | async-start | bytes 327680 | tf_op jit(solution)/shard_map/all_to_all | solution.py:71
  112.7 26.4 %collective-permute-start = (f32[2,4,128,128]{3,0,2,1:T(2,128)S(1)}, f32[2,4,128,128]{3,0,2,1:T(2,128)S(1)}, u32[]{:S(2)}, u32[]{:S(2)}) collective-permute-start(f32[2,4,128,128]{3,0,2,1:T(2,128)S(1)} %fusion.23), channel_id=1, source_target_pairs={{14,0},{0,2},{2,4},{4,6},{6,8},{8,10},{10,12},{12,14},{15,1},{1,3}... | collective-permute-start | bytes 1572872 | tf_op jit(solution)/shard_map/ppermute | solution.py:14
  113.7 1.3 copy-start.3
  115.0 22.9 %collective-permute-start.6 = (f32[2,4,128,128]{3,0,2,1:T(2,128)S(1)}, f32[2,4,128,128]{3,0,2,1:T(2,128)S(1)}, u32[]{:S(2)}, u32[]{:S(2)}) collective-permute-start(f32[2,4,128,128]{3,0,2,1:T(2,128)S(1)} %copy-done.3), channel_id=1, source_target_pairs={{2,0},{4,2},{6,4},{8,6},{10,8},{12,10},{14,12},{0,14},{3,1},{5,3},... | collective-permute-start | bytes 1572872 | tf_op jit(solution)/shard_map/ppermute | solution.py:14
  148.3 3.2 %copy-start.1 = (f32[4,4,128,128]{3,2,1,0:T(8,128)}, f32[4,4,128,128]{3,2,1,0:T(8,128)S(1)}, u32[]{:S(2)}) copy-start(f32[4,4,128,128]{3,2,1,0:T(8,128)S(1)} %copy.22) | copy-start | bytes 3145732
  150.1 0.7 copy-start.5
where the time goes:
time: 152 us
  waiting for transfers between devices  67.9 us (45%)
  matrix products  36.1 us (24%)
  starting transfers between devices  20.4 us (13%)
  blocking collectives  13.1 us (9%)
  other arithmetic  6.68 us (4%)
  local copies, waits for them, and re-layouts  5.66 us (4%)
  between operations  1.7 us (1%)
    all_to_all x1, waiting for transfers between devices, local(): lax.all_to_all(looked_gates, 'beam', split_axis=0, concat_axis=0, tiled=T...  50.1 us
    dot_general x7, matrix products, local(): jnp.einsum('cr,rhij->chij', select, states, precision=lax.Precision.HIGHEST)  16.9 us
    dot_general x7, matrix products, local(): jnp.einsum('rc,chij->rhij', placing, received, precision=lax.Precision.HI...  13.7 us
    unnamed x1, blocking collectives  13.1 us
    ppermute x7, starting transfers between devices, from_behind(): return lax.ppermute(block, axis, route)  11.3 us
    ppermute x7, waiting for transfers between devices, from_behind(): return lax.ppermute(block, axis, route)  10.4 us
    all_to_all x1, waiting for transfers between devices, local(): lax.all_to_all(looked, 'beam', split_axis=0, concat_axis=0, tiled=True)  7.32 us
    all_to_all x1, starting transfers between devices, local(): lax.all_to_all(looked_gates, 'beam', split_axis=0, concat_axis=0, tiled=T...  5.71 us
  transfers between devices with their start and end apart: 9, of which 3 were waited for; matrix products, arithmetic and copies ran while one was open for 19% of the time, Pallas kernels for 0%

commit v1 on v0

v1 whole, which is shorter than its diff:
```python
import jax
import jax.numpy as jnp
from jax import lax
from jax.experimental import pallas as pl
from jax.experimental.pallas import tpu as pltpu
from jax.sharding import PartitionSpec as P

HEAD_DIM = 128
BEAMS = 8
SPLIT = 2
AHEAD = 2
PEAK = 4.0
LEVELS = 32767.0
MESH = pl.DeviceIdType.MESH


def encode(x):
    root = jnp.sqrt(jnp.sqrt(jnp.sqrt(jnp.abs(x) * (1.0 / PEAK))))
    scaled = jnp.where(x < 0, -root, root) * LEVELS
    return jnp.round(scaled).astype(jnp.int32).astype(jnp.int16)


def decode(code):
    y = code.astype(jnp.int32).astype(jnp.float32) * (1.0 / LEVELS)
    y2 = y * y
    y4 = y2 * y2
    return (y4 * PEAK) * (y4 * jnp.where(y < 0, -1.0, 1.0))


def flip(beam, bit):
    return beam + bit - 2 * bit * lax.rem(lax.div(beam, bit), 2)


def exchange_kernel(
    n, heads, hyps, vocab, states, meta, table, picked, ent,
    own, mir, xsnd, xrcv, zsnd, zrcv, mrcv, esnd, ercv,
    send_sems, recv_sems, msend, mrecv, esend, erecv,
):
    me = lax.axis_index("beam")
    spacing = n // BEAMS
    beam = lax.div(me, spacing)
    off = lax.rem(me, spacing)

    def device(b):
        return b * spacing + off

    def peer(j):
        return lax.rem(me + j, n)

    chunks = heads * SPLIT
    rows = HEAD_DIM // SPLIT
    ids = hyps * heads

    barrier = pltpu.get_barrier_semaphore()
    for j in range(1, n):
        pl.semaphore_signal(barrier, inc=1, device_id={"beam": peer(j)}, device_id_type=MESH)

    for i in range(chunks):
        h, s = i // SPLIT, i % SPLIT
        for u in range(hyps):
            own[i, u] = encode(states[u, h, s * rows:(s + 1) * rows, :])

    pl.semaphore_wait(barrier, n - 1)

    def remote(src, dst, send, recv, to):
        return pltpu.make_async_remote_copy(
            src_ref=src, dst_ref=dst, send_sem=send, recv_sem=recv,
            device_id={"beam": to}, device_id_type=MESH,
        )

    metas = [None]
    for j in range(1, n):
        c = remote(meta, mrcv.at[j], msend.at[j], mrecv.at[j], peer(j))
        c.start()
        metas.append(c)

    across, beside, along = flip(beam, 4), flip(beam, 1), flip(beam, 2)
    diagonal = flip(beside, 2)
    first = [remote(own.at[i], mir.at[i], send_sems.at[0, i], recv_sems.at[0, i], device(across)) for i in range(chunks)]
    second = [remote(xsnd.at[i], xrcv.at[i], send_sems.at[1, i], recv_sems.at[1, i], device(beside)) for i in range(chunks)]
    third = [remote(zsnd.at[i], zrcv.at[i], send_sems.at[2, i], recv_sems.at[2, i], device(along)) for i in range(chunks)]
    for i in range(AHEAD):
        first[i].start()

    mrcv[0] = meta[...]
    for j in range(1, n):
        metas[j].wait()

    spot = lax.broadcasted_iota(jnp.int32, (ids, vocab), 1) + me * vocab
    head_of = lax.broadcasted_iota(jnp.int32, (ids, vocab), 0) // hyps
    entries = [None]
    for j in range(n):
        hit = mrcv[j, 0:ids, :] == spot
        found = jnp.zeros((ids, table.shape[2]), jnp.float32)
        for h in range(heads):
            mask = (hit & (head_of == h)).astype(jnp.float32).astype(jnp.bfloat16)
            found += jnp.dot(mask, table[h], preferred_element_type=jnp.float32)
        if j == 0:
            ercv[0] = found.astype(jnp.bfloat16)
        else:
            esnd[j] = found.astype(jnp.bfloat16)
            c = remote(esnd.at[j], ercv.at[j], esend.at[j], erecv.at[j], peer(n - j))
            c.start()
            entries.append(c)

    def parents_of(b):
        slot = lax.rem(me - device(b) + n, n)
        return mrcv[slot, ids:ids + hyps, :][:, :HEAD_DIM]

    mine = parents_of(beam)
    at_beside, at_diagonal, at_along = parents_of(beside), parents_of(diagonal), parents_of(along)

    def wide(code):
        return code.astype(jnp.int32)

    for i in range(chunks + 2):
        if i < chunks:
            first[i].wait_recv()
            if i + AHEAD < chunks:
                first[i + AHEAD].start()
            for u in range(hyps):
                a, m = wide(own[i, u]), wide(mir[i, u])
                xsnd[i, u] = jnp.where(at_beside[u:u + 1] == beam, a, m).astype(jnp.int16)
                xsnd[i, hyps + u] = jnp.where(at_diagonal[u:u + 1] == beam, a, m).astype(jnp.int16)
            second[i].start()
        if 1 <= i <= chunks:
            t = i - 1
            second[t].wait_recv()
            for u in range(hyps):
                a, m, x = wide(own[t, u]), wide(mir[t, u]), wide(xrcv[t, hyps + u])
                p = at_along[u:u + 1]
                zsnd[t, u] = jnp.where(p == beam, a, jnp.where(p == across, m, x)).astype(jnp.int16)
            third[t].start()
        if i >= 2:
            t = i - 2
            h, s = t // SPLIT, t % SPLIT
            third[t].wait_recv()
            for u in range(hyps):
                m, x, z = wide(mir[t, u]), wide(xrcv[t, u]), wide(zrcv[t, u])
                p = mine[u:u + 1]
                near = (p == beside) | (p == flip(beside, 4))
                got = jnp.where(p == across, m, jnp.where(near, x, z))
                picked[u, h, s * rows:(s + 1) * rows, :] = got.astype(jnp.int16)

    total = ercv[0].astype(jnp.float32)
    for j in range(1, n):
        entries[j].wait_recv()
        total += ercv[j].astype(jnp.float32)
    ent[...] = total
    for j in range(1, n):
        entries[j].wait_send()
    for i in range(chunks):
        first[i].wait_send()
        second[i].wait_send()
        third[i].wait_send()


def unit_norm(vector):
    return vector * lax.rsqrt(jnp.sum(vector * vector, axis=-1, keepdims=True) + 1e-06)


def update_kernel(heads, hyps, beams, states, picked, ent, gain, readout, new_states):
    d = HEAD_DIM
    query = unit_norm(ent[:, 0:d])
    keys = (unit_norm(ent[:, d:2 * d]), unit_norm(ent[:, 2 * d:3 * d]))
    values = (ent[:, 3 * d:4 * d].T, ent[:, 4 * d:5 * d].T)
    gates = jax.nn.sigmoid(ent[:, 5 * d:6 * d])
    lane = lax.broadcasted_iota(jnp.int32, (d, heads * hyps), 1)
    outs = jnp.zeros((d, heads * hyps), jnp.float32)
    my_beam = beams[hyps]
    for h in range(heads):
        for u in range(hyps):
            i = h * hyps + u
            now = jnp.where(beams[u] == my_beam, states[u, h], decode(picked[u, h]))
            now = gates[i:i + 1, 0:1] * now
            for j in range(2):
                key = keys[j][i:i + 1, :]
                applied = jnp.sum(now * key, axis=1, keepdims=True)
                step = (2.0 * gates[i:i + 1, 1 + j:2 + j]) * (applied - values[j][:, i:i + 1])
                now = now - step * key
            new_states[u, h] = now
            out = jnp.sum(now * query[i:i + 1, :], axis=1, keepdims=True)
            outs = jnp.where(lane == i, out, outs)
    rows = outs.T
    rows = rows * lax.rsqrt(jnp.mean(rows * rows, axis=-1, keepdims=True) + 1e-05)
    for h in range(heads):
        for u in range(hyps):
            i = h * hyps + u
            readout[u, h:h + 1, :] = (gain[h:h + 1, :] * rows[i:i + 1, :]).astype(jnp.bfloat16)


def local(states, parent_beam, next_token, proj_table, gate_table, gain):
    hyps, heads = states.shape[:2]
    vocab = proj_table.shape[0]
    n = lax.axis_size("beam")
    ids = hyps * heads
    my_beam = lax.axis_index("beam") // (n // BEAMS)
    chunks, rows = heads * SPLIT, HEAD_DIM // SPLIT
    column = jnp.concatenate([jnp.tile(next_token, heads), parent_beam, jnp.zeros((-(ids + hyps) % 8,), jnp.int32)])
    meta = jnp.broadcast_to(column[:, None], (column.shape[0], vocab))
    gates = jnp.pad(jnp.transpose(gate_table, (2, 0, 1)), ((0, 0), (0, 0), (0, HEAD_DIM - 3)))
    table = jnp.concatenate([jnp.transpose(proj_table, (1, 0, 2)), gates], axis=2)
    width = table.shape[2]
    vmem = pl.BlockSpec(memory_space=pltpu.VMEM)

    def codes(slots):
        return pltpu.VMEM((chunks, slots, rows, HEAD_DIM), jnp.int16)

    dma = pltpu.SemaphoreType.DMA
    picked, ent = pl.pallas_call(
        lambda *refs: exchange_kernel(n, heads, hyps, vocab, *refs),
        out_shape=(
            jax.ShapeDtypeStruct(states.shape, jnp.int16),
            jax.ShapeDtypeStruct((ids, width), jnp.float32),
        ),
        in_specs=[vmem] * 3,
        out_specs=(vmem, vmem),
        scratch_shapes=[
            codes(hyps), codes(hyps), codes(2 * hyps), codes(2 * hyps), codes(hyps), codes(hyps),
            pltpu.VMEM((n,) + meta.shape, jnp.int32),
            pltpu.VMEM((n, ids, width), jnp.bfloat16),
            pltpu.VMEM((n, ids, width), jnp.bfloat16),
            dma((3, chunks)), dma((3, chunks)), dma((n,)), dma((n,)), dma((n,)), dma((n,)),
        ],
        compiler_params=pltpu.CompilerParams(collective_id=0, has_side_effects=True),
        name="exchange",
    )(states, meta, table)
    beams = jnp.concatenate([parent_beam, my_beam[None].astype(jnp.int32)])
    return pl.pallas_call(
        lambda *refs: update_kernel(heads, hyps, refs[0], *refs[1:]),
        out_shape=(
            jax.ShapeDtypeStruct((hyps, heads, HEAD_DIM), jnp.bfloat16),
            jax.ShapeDtypeStruct(states.shape, jnp.float32),
        ),
        in_specs=[pl.BlockSpec(memory_space=pltpu.SMEM)] + [vmem] * 4,
        out_specs=(vmem, vmem),
        name="update",
    )(beams, states, picked, ent, gain)


def solution(mesh):
    return jax.shard_map(
        local,
        mesh=mesh,
        in_specs=(
            P(("groups", "beam"), "mp", None, None),
            P(("groups", "beam")),
            P(("groups", "beam")),
            P("beam", "mp", None),
            P("beam", None, "mp"),
            P("mp", None),
        ),
        out_specs=(P(("groups", "beam"), "mp", None), P(("groups", "beam"), "mp", None, None)),
        check_vma=False,
    )
```

time: 152 us -> 64.8 us (0.43)
  waiting for transfers between devices: 67.9 us -> 0 us
  Pallas kernels: 0 us -> 57.5 us
  matrix products: 36.1 us -> 0 us
  starting transfers between devices: 20.4 us -> 0 us
  blocking collectives: 13.1 us -> 0 us
  other arithmetic: 6.68 us -> 2.99 us
  local copies, waits for them, and re-layouts: 5.66 us -> 3.43 us
    pallas_call x0 -> x2, Pallas kernels: none -> 57.5 us  [the longest x1 48.8 us: local(): pl.pallas_call(lambda *refs: exchange_kernel(n, heads, hyps, vocab, *refs...]
    all_to_all x2 -> x0, waiting for transfers between devices: 57.5 us -> none  [the longest x1 50.1 us: local(): lax.all_to_all(looked_gates, 'beam', split_axis=0, concat_axis=0, tiled=T...]
    dot_general x19 -> x0, matrix products: 36.1 us -> none  [the longest x7 16.9 us: local(): jnp.einsum('cr,rhij->chij', select, states, precision=lax.Precision.HIGHEST)]
    unnamed x1 -> x0, blocking collectives: 13.1 us -> none
    ppermute x7 -> x0, starting transfers between devices: 11.3 us -> none  [from_behind(): return lax.ppermute(block, axis, route)]
    ppermute x7 -> x0, waiting for transfers between devices: 10.4 us -> none  [from_behind(): return lax.ppermute(block, axis, route)]
    all_to_all x2 -> x0, starting transfers between devices: 9.1 us -> none  [the longest x1 5.71 us: local(): lax.all_to_all(looked_gates, 'beam', split_axis=0, concat_axis=0, tiled=T...]
    concatenate x0 -> x3, other arithmetic: none -> 2.99 us  [the longest x1 1.3 us: local(): beams = jnp.concatenate([parent_beam, my_beam[None].astype(jnp.int32)])]
  transfers between devices with their start and end apart: 9 -> 0, of which waited for: 3 -> 0; matrix products, arithmetic and copies ran while one was open for 19% -> 0% of each run, Pallas kernels for 0% -> 0%
where the time goes in v1:
time: 64.8 us; the launch traced here: 64.6 us
  Pallas kernels  57.5 us (89%)
  local copies, waits for them, and re-layouts  3.43 us (5%)
  other arithmetic  2.99 us (5%)
  between operations  0.65 us (1%)
    pallas_call x1, Pallas kernels, local(): pl.pallas_call(lambda *refs: exchange_kernel(n, heads, hyps, vocab, *refs...  48.8 us
    pallas_call x1, Pallas kernels, local(): pl.pallas_call(lambda *refs: update_kernel(heads, hyps, refs[0], *refs[1:...  8.72 us
    unnamed x2, local copies, waits for them, and re-layouts  2.02 us
    concatenate x1, other arithmetic, local(): beams = jnp.concatenate([parent_beam, my_beam[None].astype(jnp.int32)])  1.3 us

profile of v1, /device:TPU:0, one launch (start us, length us, event | category | flops | bytes accessed | tf_op | source)
XLA Modules:
  0.0 64.6 jit_solution(16825601135974413732)
XLA Ops:
  0.6 1.3 %pad_add_fusion.refs_0_ = s32[5]{0:T(128)} fusion(s32[1]{0:T(128)} %bitcast, s32[4]{0:T(128)} %param.7), kind=kLoop, calls=%fused_computation.4 | loop fusion | flops 5 | bytes 40 | tf_op jit(solution)/shard_map/concatenate | solution.py:228
  1.9 0.7 %tile.4 = s32[4,4]{1,0:T(4,128)S(1)} broadcast(s32[4]{0:T(128)} %param.8), dimensions={1} | broadcast | bytes 80 | tf_op jit(solution)/shard_map/tile | solution.py:199
  2.6 0.1 tile.10
  2.7 0.7 %pad_add_fusion.1 = s32[24]{0:T(128)S(1)} fusion(s32[4]{0:T(128)S(1)} %broadcast.8, s32[4]{0:T(128)} %param.7, s32[16]{0:T(128)S(1)} %tile.10), kind=kLoop, calls=%fused_computation.5 | loop fusion | flops 48 | bytes 192 | tf_op jit(solution)/shard_map/concatenate | solution.py:199
  3.4 0.7 %broadcast_in_dim.10.refs_1_ = s32[24,128]{1,0:T(8,128)} broadcast(s32[24]{0:T(128)S(1)} %pad_add_fusion.1), dimensions={0} | broadcast | bytes 12384 | tf_op jit(solution)/shard_map/broadcast_in_dim | solution.py:200
  4.1 0.9 %copy.9 = bf16[128,3,4]{1,0,2:T(8,128)(2,1)S(1)} copy(bf16[128,3,4]{0,2,1:T(4,128)(2,1)} %param.10) | data formatting | bytes 6144 | tf_op args[4]
  4.9 1.2 %copy.11 = bf16[128,4,640]{2,0,1:T(8,128)(2,1)S(1)} copy(bf16[128,4,640]{2,1,0:T(4,128)(2,1)} %param.9) | data formatting | bytes 1310720 | tf_op args[3]
  6.1 0.9 %fusion.1.refs_2_ = bf16[4,128,768]{2,1,0:T(8,128)(2,1)} fusion(bf16[4,128,3]{2,1,0:T(8,128)(2,1)S(1)} %bitcast.6, bf16[4,128,640]{2,1,0:T(8,128)(2,1)S(1)} %bitcast.5), kind=kLoop, calls=%fused_computation.2 | loop fusion | flops 2359296 | bytes 1444864 | tf_op jit(solution)/shard_map/concatenate | solution.py:202
  7.1 48.8 %exchange.1 = (s16[4,4,128,128]{3,2,1,0:T(8,128)(2,1)}, f32[16,768]{1,0:T(8,128)}) custom-call(f32[4,4,128,128]{3,2,1,0:T(8,128)} %refs_1_.1, s32[24,128]{1,0:T(8,128)} %broadcast_in_dim.10.refs_1_, bf16[4,128,768]{2,1,0:T(8,128)(2,1)} %fusion.1.refs_2_), custom_call_target="tpu_custom_call" | custom-call | tf_op jit(solution)/shard_map/exchange/pallas_call | solution.py:210
  55.8 8.7 %update.1 = (bf16[4,4,128]{2,1,0:T(4,128)(2,1)}, f32[4,4,128,128]{3,2,1,0:T(8,128)}) custom-call(s32[5]{0:T(128)} %pad_add_fusion.refs_0_, f32[4,4,128,128]{3,2,1,0:T(8,128)} %refs_1_.1, s16[4,4,128,128]{3,2,1,0:T(8,128)(2,1)} %get-tuple-element.4.refs_2_, f32[16,768]{1,0:T(8,128)} %get-tuple-element.5.refs_3_, f32[4,128]{1,0:T(4,128)} %refs_4_.1), custom_call_target="tpu_custom_call" | custom-call | tf_op jit(solution)/shard_map/update/pallas_call | solution.py:229
  (1 shorter events, 0.0 us)

commit v2 on v1

v2 whole, which is shorter than its diff:
```python
import jax
import jax.numpy as jnp
from jax import lax
from jax.experimental import pallas as pl
from jax.experimental.pallas import tpu as pltpu
from jax.sharding import PartitionSpec as P

HEAD_DIM = 128
BEAMS = 8
SPLIT = 2
AHEAD = 3
PEAK = 4.0
LEVELS = 32767.0
MESH = pl.DeviceIdType.MESH


def encode(x):
    root = jnp.sqrt(jnp.sqrt(jnp.sqrt(jnp.abs(x) * (1.0 / PEAK))))
    scaled = jnp.where(x < 0, -root, root) * LEVELS
    return jnp.round(scaled).astype(jnp.int32).astype(jnp.int16)


def decode(code):
    y = code.astype(jnp.int32).astype(jnp.float32) * (1.0 / LEVELS)
    y2 = y * y
    y4 = y2 * y2
    return (y4 * PEAK) * (y4 * jnp.where(y < 0, -1.0, 1.0))


def flip(beam, bit):
    return beam + bit - 2 * bit * lax.rem(lax.div(beam, bit), 2)


def unit_norm(vector):
    return vector * lax.rsqrt(jnp.sum(vector * vector, axis=-1, keepdims=True) + 1e-06)


def step_kernel(
    n, heads, hyps, vocab, states, token, parent, table, gate, gain, readout, new_states,
    held, own, mir, xsnd, xrcv, zsnd, zrcv, mloc, mrcv, esnd, ercv, fresh,
    send_sems, recv_sems, msend, mrecv, esend, erecv, load_sems, store_sems,
):
    me = lax.axis_index("beam")
    spacing = n // BEAMS
    beam = lax.div(me, spacing)
    off = lax.rem(me, spacing)
    d = HEAD_DIM

    def device(b):
        return b * spacing + off

    def peer(j):
        return lax.rem(me + j, n)

    chunks = heads * SPLIT
    rows = d // SPLIT
    ids = hyps * heads

    loads = [pltpu.make_async_copy(states.at[:, h], held.at[h], load_sems.at[h]) for h in range(heads)]
    for c in loads:
        c.start()
    barrier = pltpu.get_barrier_semaphore()
    for j in range(1, n):
        pl.semaphore_signal(barrier, inc=1, device_id={"beam": peer(j)}, device_id_type=MESH)

    mloc[...] = jnp.zeros(mloc.shape, jnp.int32)
    for h in range(heads):
        mloc[:, h * hyps:(h + 1) * hyps] = token[...] * heads + h
    mloc[:, ids:ids + hyps] = parent[...]

    def encode_head(h):
        loads[h].wait()
        for s in range(SPLIT):
            for u in range(hyps):
                own[h * SPLIT + s, u] = encode(held[h, u, s * rows:(s + 1) * rows, :])

    encode_head(0)
    pl.semaphore_wait(barrier, n - 1)

    def remote(src, dst, send, recv, to):
        return pltpu.make_async_remote_copy(
            src_ref=src, dst_ref=dst, send_sem=send, recv_sem=recv,
            device_id={"beam": to}, device_id_type=MESH,
        )

    metas = [None]
    for j in range(1, n):
        c = remote(mloc, mrcv.at[j], msend.at[j], mrecv.at[j], peer(j))
        c.start()
        metas.append(c)

    across, beside, along = flip(beam, 4), flip(beam, 1), flip(beam, 2)
    diagonal = flip(beside, 2)
    first = [remote(own.at[i], mir.at[i], send_sems.at[0, i], recv_sems.at[0, i], device(across)) for i in range(chunks)]
    second = [remote(xsnd.at[i], xrcv.at[i], send_sems.at[1, i], recv_sems.at[1, i], device(beside)) for i in range(chunks)]
    third = [remote(zsnd.at[i], zrcv.at[i], send_sems.at[2, i], recv_sems.at[2, i], device(along)) for i in range(chunks)]
    started = 0
    while started < min(AHEAD, SPLIT):
        first[started].start()
        started += 1
    for h in range(1, heads):
        encode_head(h)
        while started < min(AHEAD, (h + 1) * SPLIT):
            first[started].start()
            started += 1

    mrcv[0] = mloc[...]
    for j in range(1, n):
        metas[j].wait()

    keys_of = jnp.concatenate([mrcv[j] for j in range(n)], axis=0).T
    spot = lax.broadcasted_iota(jnp.int32, (ids, vocab * heads), 1) + me * (vocab * heads)
    gate_spot = lax.broadcasted_iota(jnp.int32, (ids, vocab), 1) + me * vocab
    head_of = lax.broadcasted_iota(jnp.int32, (ids, 1), 0) // hyps
    head_lane = lax.broadcasted_iota(jnp.int32, (ids, heads), 1) == head_of
    lane = lax.broadcasted_iota(jnp.int32, (ids, d), 1)
    flat = table[...].reshape(vocab * heads, 5 * d)
    entries = [None]
    for j in range(n):
        key = keys_of[0:ids, j:j + 1]
        hit = (key == spot).astype(jnp.float32).astype(jnp.bfloat16)
        found = jnp.dot(hit, flat, preferred_element_type=jnp.float32).astype(jnp.bfloat16)
        word = (key - head_of == gate_spot * heads).astype(jnp.float32).astype(jnp.bfloat16)
        gates = jnp.zeros((ids, d), jnp.float32)
        for g in range(3):
            every = lax.dot_general(word, gate[g], (((1,), (1,)), ((), ())), preferred_element_type=jnp.float32)
            one = jnp.sum(jnp.where(head_lane, every, 0.0), axis=1, keepdims=True)
            gates = jnp.where(lane == g, one, gates)
        to = ercv.at[0] if j == 0 else esnd.at[j]
        to[:, 0:5 * d] = found
        to[:, 5 * d:6 * d] = gates.astype(jnp.bfloat16)
        if j > 0:
            c = remote(esnd.at[j], ercv.at[j], esend.at[j], erecv.at[j], peer(n - j))
            c.start()
            entries.append(c)

    place = lax.broadcasted_iota(jnp.int32, (1, d), 1)

    def parents_of(b):
        row = mrcv[lax.rem(me - device(b) + n, n)]
        return [jnp.broadcast_to(jnp.sum(jnp.where(place == ids + u, row, 0), axis=1, keepdims=True), (1, d)) for u in range(hyps)]

    mine = parents_of(beam)
    at_beside, at_diagonal, at_along = parents_of(beside), parents_of(diagonal), parents_of(along)

    def wide(code):
        return code.astype(jnp.int32)

    stores = []
    outs = [jnp.zeros((rows, d), jnp.float32) for s in range(SPLIT)]
    out_lane = lax.broadcasted_iota(jnp.int32, (rows, d), 1)
    for i in range(chunks + 2):
        if i < chunks:
            first[i].wait_recv()
            if started < chunks:
                first[started].start()
                started += 1
            for u in range(hyps):
                a, m = wide(own[i, u]), wide(mir[i, u])
                xsnd[i, u] = jnp.where(at_beside[u] == beam, a, m).astype(jnp.int16)
                xsnd[i, hyps + u] = jnp.where(at_diagonal[u] == beam, a, m).astype(jnp.int16)
            second[i].start()
        if 1 <= i <= chunks:
            t = i - 1
            second[t].wait_recv()
            for u in range(hyps):
                a, m, x = wide(own[t, u]), wide(mir[t, u]), wide(xrcv[t, hyps + u])
                p = at_along[u]
                zsnd[t, u] = jnp.where(p == beam, a, jnp.where(p == across, m, x)).astype(jnp.int16)
            third[t].start()
        if i == 2:
            total = ercv[0].astype(jnp.float32)
            for j in range(1, n):
                entries[j].wait_recv()
                total += ercv[j].astype(jnp.float32)
            query = unit_norm(total[:, 0:d])
            keys = (unit_norm(total[:, d:2 * d]), unit_norm(total[:, 2 * d:3 * d]))
            values = (total[:, 3 * d:4 * d].T, total[:, 4 * d:5 * d].T)
            gates = jax.nn.sigmoid(total[:, 5 * d:6 * d])
        if i >= 2:
            t = i - 2
            h, s = t // SPLIT, t % SPLIT
            part = slice(s * rows, (s + 1) * rows)
            third[t].wait_recv()
            for u in range(hyps):
                m, x, z = wide(mir[t, u]), wide(xrcv[t, u]), wide(zrcv[t, u])
                p = mine[u]
                near = (p == beside) | (p == flip(beside, 4))
                got = decode(jnp.where(p == across, m, jnp.where(near, x, z)))
                k = h * hyps + u
                now = gates[k:k + 1, 0:1] * jnp.where(p == beam, held[h, u, part, :], got)
                for j in range(2):
                    key = keys[j][k:k + 1, :]
                    applied = jnp.sum(now * key, axis=1, keepdims=True)
                    now = now - (2.0 * gates[k:k + 1, 1 + j:2 + j]) * (applied - values[j][part, k:k + 1]) * key
                fresh[t, u] = now
                out = jnp.sum(now * query[k:k + 1, :], axis=1, keepdims=True)
                outs[s] = jnp.where(out_lane == k, out, outs[s])
            c = pltpu.make_async_copy(fresh.at[t], new_states.at[:, h, part, :], store_sems.at[t])
            c.start()
            stores.append(c)

    out_rows = jnp.concatenate(outs, axis=0).T[0:ids]
    out_rows = out_rows * lax.rsqrt(jnp.mean(out_rows * out_rows, axis=-1, keepdims=True) + 1e-05)
    for h in range(heads):
        for u in range(hyps):
            k = h * hyps + u
            readout[u, h:h + 1, :] = (gain[h:h + 1, :] * out_rows[k:k + 1, :]).astype(jnp.bfloat16)
    for j in range(1, n):
        entries[j].wait_send()
    for i in range(chunks):
        first[i].wait_send()
        second[i].wait_send()
        third[i].wait_send()
        stores[i].wait()


def local(states, parent_beam, next_token, proj_table, gate_table, gain):
    hyps, heads = states.shape[:2]
    vocab = proj_table.shape[0]
    n = lax.axis_size("beam")
    ids = hyps * heads
    chunks, rows = heads * SPLIT, HEAD_DIM // SPLIT
    width = 6 * HEAD_DIM
    vmem = pl.BlockSpec(memory_space=pltpu.VMEM)
    hbm = pl.BlockSpec(memory_space=pl.ANY)

    def codes(slots):
        return pltpu.VMEM((chunks, slots, rows, HEAD_DIM), jnp.int16)

    dma = pltpu.SemaphoreType.DMA
    return pl.pallas_call(
        lambda *refs: step_kernel(n, heads, hyps, vocab, *refs),
        out_shape=(
            jax.ShapeDtypeStruct((hyps, heads, HEAD_DIM), jnp.bfloat16),
            jax.ShapeDtypeStruct(states.shape, jnp.float32),
        ),
        in_specs=[hbm] + [vmem] * 5,
        out_specs=(vmem, hbm),
        scratch_shapes=[
            pltpu.VMEM((heads, hyps, HEAD_DIM, HEAD_DIM), jnp.float32),
            codes(hyps), codes(hyps), codes(2 * hyps), codes(2 * hyps), codes(hyps), codes(hyps),
            pltpu.VMEM((1, HEAD_DIM), jnp.int32),
            pltpu.VMEM((n, 1, HEAD_DIM), jnp.int32),
            pltpu.VMEM((n, ids, width), jnp.bfloat16),
            pltpu.VMEM((n, ids, width), jnp.bfloat16),
            pltpu.VMEM((chunks, hyps, rows, HEAD_DIM), jnp.float32),
            dma((3, chunks)), dma((3, chunks)), dma((n,)), dma((n,)), dma((n,)), dma((n,)),
            dma((heads,)), dma((chunks,)),
        ],
        compiler_params=pltpu.CompilerParams(collective_id=0, has_side_effects=True),
        name="step",
    )(
        states, next_token.reshape(1, hyps), parent_beam.reshape(1, hyps), proj_table,
        jnp.transpose(gate_table, (1, 2, 0)), gain,
    )


def solution(mesh):
    return jax.shard_map(
        local,
        mesh=mesh,
        in_specs=(
            P(("groups", "beam"), "mp", None, None),
            P(("groups", "beam")),
            P(("groups", "beam")),
            P("beam", "mp", None),
            P("beam", None, "mp"),
            P("mp", None),
        ),
        out_specs=(P(("groups", "beam"), "mp", None), P(("groups", "beam"), "mp", None, None)),
        check_vma=False,
    )
```

time: 64.8 us -> 53.2 us (0.82)
  Pallas kernels: 57.5 us -> 48.8 us
  other arithmetic: 2.99 us -> 0 us
    pallas_call x2 -> x1, Pallas kernels: 57.5 us -> 48.8 us  [local(): pl.pallas_call(lambda *refs: step_kernel(n, heads, hyps, vocab, *refs), o...]
    concatenate x3 -> x0, other arithmetic: 2.99 us -> none  [the longest x1 1.3 us: local(): beams = jnp.concatenate([parent_beam, my_beam[None].astype(jnp.int32)])]
    unnamed x2, local copies, waits for them, and re-layouts: 2.02 us -> 3.57 us
    another operation x3 -> x0, local copies, waits for them, and re-layouts: 0.74 us -> none  [the longest x2 0.74 us: local(): jnp.tile(next_token, heads)]
    broadcast_in_dim x1 -> x0, local copies, waits for them, and re-layouts: 0.67 us -> none  [local(): meta = jnp.broadcast_to(column[:, None], (column.shape[0], vocab))]
where the time goes in v2:
time: 53.2 us; the launch traced here: 53 us
  Pallas kernels  48.8 us (92%)
  local copies, waits for them, and re-layouts  3.57 us (7%)
  between operations  0.64 us (1%)
    pallas_call x1, Pallas kernels, local(): pl.pallas_call(lambda *refs: step_kernel(n, heads, hyps, vocab, *refs), o...  48.8 us
    unnamed x2, local copies, waits for them, and re-layouts  3.57 us

profile of v2, /device:TPU:0, one launch (start us, length us, event | category | flops | bytes accessed | tf_op | source)
XLA Modules:
  0.0 53.0 jit_solution(874026144519452110)
XLA Ops:
  0.6 48.8 %step.1 = (bf16[4,4,128]{2,1,0:T(4,128)(2,1)}, f32[4,4,128,128]{3,2,1,0:T(8,128)}) custom-call(f32[4,4,128,128]{3,2,1,0:T(8,128)} %refs_0_.1, s32[1,4]{1,0:T(1,128)} %bitcast.4, s32[1,4]{1,0:T(1,128)} %bitcast.5, bf16[128,4,640]{2,1,0:T(4,128)(2,1)} %refs_3_.1, bf16[3,4,128]{2,1,0:T(4,128)(2,1)} %bitcast.3, f32[4,128]{1,0:T(4,128)} %refs_5_.1), custom_call_target="tpu_custom_call" | custom-call | tf_op jit(solution)/shard_map/step/pallas_call | solution.py:232
  49.4 1.3 %copy.10 = bf16[4,4,128]{2,1,0:T(4,128)(2,1)} copy(bf16[4,4,128]{2,1,0:T(4,128)(2,1)} %get-tuple-element.4) | data formatting | bytes 8192
  50.7 2.3 %copy.11 = f32[4,4,128,128]{3,2,1,0:T(8,128)} copy(f32[4,4,128,128]{3,2,1,0:T(8,128)} %get-tuple-element.5) | data formatting | bytes 2097152

commit v3 on v2

v3 whole, which is shorter than its diff:
```python
import jax
import jax.numpy as jnp
from jax import lax
from jax.experimental import pallas as pl
from jax.experimental.pallas import tpu as pltpu
from jax.sharding import PartitionSpec as P

HEAD_DIM = 128
BEAMS = 8
SPLIT = 2
AHEAD = 3
LAG = 2
PEAK = 4.0
LEVELS = 32767.0
MESH = pl.DeviceIdType.MESH


def encode(x):
    root = jnp.sqrt(jnp.sqrt(jnp.sqrt(jnp.abs(x) * (1.0 / PEAK))))
    scaled = jnp.where(x < 0, -root, root) * LEVELS
    return jnp.round(scaled).astype(jnp.int32).astype(jnp.int16)


def decode(code):
    y = code.astype(jnp.int32).astype(jnp.float32) * (1.0 / LEVELS)
    y2 = y * y
    y4 = y2 * y2
    return (y4 * PEAK) * (y4 * jnp.where(y < 0, -1.0, 1.0))


def flip(beam, bit):
    return beam + bit - 2 * bit * lax.rem(lax.div(beam, bit), 2)


def unit_norm(vector):
    return vector * lax.rsqrt(jnp.sum(vector * vector, axis=-1, keepdims=True) + 1e-06)


def step_kernel(
    n, heads, hyps, vocab, states, token, parent, table, gate, gain, readout, new_states,
    held, own, mir, xsnd, xrcv, zsnd, zrcv, mloc, mrcv, esnd, ercv, fresh,
    keys, columns, strengths, outs,
    send_sems, recv_sems, msend, mrecv, esend, erecv, load_sems, store_sems,
):
    me = lax.axis_index("beam")
    spacing = n // BEAMS
    beam = lax.div(me, spacing)
    off = lax.rem(me, spacing)
    d = HEAD_DIM
    chunks = heads * SPLIT
    rows = d // SPLIT
    ids = hyps * heads

    def device(b):
        return b * spacing + off

    def peer(j):
        return lax.rem(me + j, n)

    def repeat(low, high, body):
        def step(i, carry):
            body(i)
            return carry
        lax.fori_loop(low, high, step, 0)

    def remote(src, dst, send, recv, to):
        return pltpu.make_async_remote_copy(
            src_ref=src, dst_ref=dst, send_sem=send, recv_sem=recv,
            device_id={"beam": to}, device_id_type=MESH,
        )

    across, beside, along = flip(beam, 4), flip(beam, 1), flip(beam, 2)
    diagonal = flip(beside, 2)

    def load(h):
        return pltpu.make_async_copy(states.at[:, h], held.at[h], load_sems.at[h])

    def first(i):
        return remote(own.at[i], mir.at[i], send_sems.at[0, i], recv_sems.at[0, i], device(across))

    def second(i):
        return remote(xsnd.at[i], xrcv.at[i], send_sems.at[1, i], recv_sems.at[1, i], device(beside))

    def third(i):
        return remote(zsnd.at[i], zrcv.at[i], send_sems.at[2, i], recv_sems.at[2, i], device(along))

    def note(j):
        return remote(mloc, mrcv.at[j], msend.at[j], mrecv.at[j], peer(j))

    def entry(j):
        return remote(esnd.at[j], ercv.at[j], esend.at[j], erecv.at[j], peer(n - j))

    def store(i):
        h, part = lax.div(i, SPLIT), pl.ds(lax.rem(i, SPLIT) * rows, rows)
        return pltpu.make_async_copy(fresh.at[i], new_states.at[:, h, part, :], store_sems.at[i])

    for h in range(heads):
        load(h).start()
    barrier = pltpu.get_barrier_semaphore()

    def greet(j):
        pl.semaphore_signal(barrier, inc=1, device_id={"beam": peer(j)}, device_id_type=MESH)

    repeat(1, n, greet)

    mloc[...] = jnp.zeros(mloc.shape, jnp.int32)
    for h in range(heads):
        mloc[:, h * hyps:(h + 1) * hyps] = token[...] * heads + h
    mloc[:, ids:ids + hyps] = parent[...]

    def encode_chunk(i):
        h, s = lax.div(i, SPLIT), lax.rem(i, SPLIT)

        @pl.when(s == 0)
        def _():
            load(h).wait()

        for u in range(hyps):
            own[i, u] = encode(held[h, u, pl.ds(s * rows, rows), :])

    repeat(0, AHEAD, encode_chunk)
    pl.semaphore_wait(barrier, n - 1)
    repeat(1, n, lambda j: note(j).start())
    for i in range(AHEAD):
        first(i).start()
    repeat(AHEAD, chunks, encode_chunk)
    mrcv[0] = mloc[...]
    repeat(1, n, lambda j: note(j).wait())

    spot = lax.broadcasted_iota(jnp.int32, (ids, vocab * heads), 1) + me * (vocab * heads)
    gate_spot = lax.broadcasted_iota(jnp.int32, (ids, vocab), 1) + me * vocab
    head_of = lax.broadcasted_iota(jnp.int32, (ids, 1), 0) // hyps
    head_lane = lax.broadcasted_iota(jnp.int32, (ids, heads), 1) == head_of
    lane = lax.broadcasted_iota(jnp.int32, (ids, d), 1)
    flat = table[...].reshape(vocab * heads, 5 * d)

    def find(j):
        key = jnp.broadcast_to(mrcv[j], (8, d)).T[0:ids, 0:1]
        hit = (key == spot).astype(jnp.float32).astype(jnp.bfloat16)
        esnd[j, :, 0:5 * d] = jnp.dot(hit, flat, preferred_element_type=jnp.float32).astype(jnp.bfloat16)
        word = (key - head_of == gate_spot * heads).astype(jnp.float32).astype(jnp.bfloat16)
        gates = jnp.zeros((ids, d), jnp.float32)
        for g in range(3):
            every = lax.dot_general(word, gate[g], (((1,), (1,)), ((), ())), preferred_element_type=jnp.float32)
            one = jnp.sum(jnp.where(head_lane, every, 0.0), axis=1, keepdims=True)
            gates = jnp.where(lane == g, one, gates)
        esnd[j, :, 5 * d:6 * d] = gates.astype(jnp.bfloat16)

        @pl.when(j > 0)
        def _():
            entry(j).start()

    repeat(0, n, find)

    place = lax.broadcasted_iota(jnp.int32, (1, d), 1)

    def parents_of(b):
        row = mrcv[lax.rem(me - device(b) + n, n)]
        return [jnp.broadcast_to(jnp.sum(jnp.where(place == ids + u, row, 0), axis=1, keepdims=True), (1, d)) for u in range(hyps)]

    mine = parents_of(beam)
    at_beside, at_diagonal, at_along = parents_of(beside), parents_of(diagonal), parents_of(along)

    def wide(code):
        return code.astype(jnp.int32)

    out_lane = lax.broadcasted_iota(jnp.int32, (rows, d), 1)
    outs[...] = jnp.zeros(outs.shape, jnp.float32)

    def prepare():
        def add(j, total):
            entry(j).wait_recv()
            return total + ercv[j].astype(jnp.float32)

        total = lax.fori_loop(1, n, add, esnd[0].astype(jnp.float32))
        for part in range(3):
            keys[part] = unit_norm(total[:, part * d:(part + 1) * d])
        sigmoids = jax.nn.sigmoid(total[:, 5 * d:6 * d])
        for g in range(3):
            strengths[g] = jnp.broadcast_to(sigmoids[:, g:g + 1] * (1.0 if g == 0 else 2.0), (ids, d))
        for j in range(2):
            value = total[:, (3 + j) * d:(4 + j) * d].T
            for h in range(heads):
                for s in range(SPLIT):
                    columns[j, h * SPLIT + s, :, 0:hyps] = value[s * rows:(s + 1) * rows, h * hyps:(h + 1) * hyps]

    def advance(i):
        @pl.when(i < chunks)
        def _():
            first(i).wait_recv()

            @pl.when(i + AHEAD < chunks)
            def _():
                first(i + AHEAD).start()

            for u in range(hyps):
                a, m = wide(own[i, u]), wide(mir[i, u])
                xsnd[i, u] = jnp.where(at_beside[u] == beam, a, m).astype(jnp.int16)
                xsnd[i, hyps + u] = jnp.where(at_diagonal[u] == beam, a, m).astype(jnp.int16)
            second(i).start()

        t = i - LAG

        @pl.when((t >= 0) & (t < chunks))
        def _():
            second(t).wait_recv()
            for u in range(hyps):
                a, m, x = wide(own[t, u]), wide(mir[t, u]), wide(xrcv[t, hyps + u])
                p = at_along[u]
                zsnd[t, u] = jnp.where(p == beam, a, jnp.where(p == across, m, x)).astype(jnp.int16)
            third(t).start()

        f = i - 2 * LAG

        @pl.when(f == 0)
        def _():
            prepare()

        @pl.when(f >= 0)
        def _():
            h, s = lax.div(f, SPLIT), lax.rem(f, SPLIT)
            third(f).wait_recv()
            for u in range(hyps):
                m, x, z = wide(mir[f, u]), wide(xrcv[f, u]), wide(zrcv[f, u])
                p = mine[u]
                near = (p == beside) | (p == flip(beside, 4))
                got = decode(jnp.where(p == across, m, jnp.where(near, x, z)))
                row = pl.ds(h * hyps + u, 1)
                now = strengths[0, row, :] * jnp.where(p == beam, held[h, u, pl.ds(s * rows, rows), :], got)
                for j in range(2):
                    key = keys[1 + j, row, :]
                    applied = jnp.sum(now * key, axis=1, keepdims=True)
                    now = now - (applied - columns[j, f, :, u:u + 1]) * (strengths[1 + j, row, :] * key)
                fresh[f, u] = now
                out = jnp.sum(now * keys[0, row, :], axis=1, keepdims=True)
                outs[s] = jnp.where(out_lane == h * hyps + u, out, outs[s])
            store(f).start()

    repeat(0, chunks + 2 * LAG, advance)

    out_rows = outs[...].reshape(d, d).T[0:ids]
    out_rows = out_rows * lax.rsqrt(jnp.mean(out_rows * out_rows, axis=-1, keepdims=True) + 1e-05)
    for h in range(heads):
        for u in range(hyps):
            k = h * hyps + u
            readout[u, h:h + 1, :] = (gain[h:h + 1, :] * out_rows[k:k + 1, :]).astype(jnp.bfloat16)
    repeat(1, n, lambda j: entry(j).wait_send())

    def finish(i):
        first(i).wait_send()
        second(i).wait_send()
        third(i).wait_send()
        store(i).wait()

    repeat(0, chunks, finish)


def local(states, parent_beam, next_token, proj_table, gate_table, gain):
    hyps, heads = states.shape[:2]
    vocab = proj_table.shape[0]
    n = lax.axis_size("beam")
    ids = hyps * heads
    chunks, rows = heads * SPLIT, HEAD_DIM // SPLIT
    width = 6 * HEAD_DIM
    vmem = pl.BlockSpec(memory_space=pltpu.VMEM)
    hbm = pl.BlockSpec(memory_space=pl.ANY)

    def codes(slots):
        return pltpu.VMEM((chunks, slots, rows, HEAD_DIM), jnp.int16)

    dma = pltpu.SemaphoreType.DMA
    return pl.pallas_call(
        lambda *refs: step_kernel(n, heads, hyps, vocab, *refs),
        out_shape=(
            jax.ShapeDtypeStruct((hyps, heads, HEAD_DIM), jnp.bfloat16),
            jax.ShapeDtypeStruct(states.shape, jnp.float32),
        ),
        in_specs=[hbm] + [vmem] * 5,
        out_specs=(vmem, hbm),
        scratch_shapes=[
            pltpu.VMEM((heads, hyps, HEAD_DIM, HEAD_DIM), jnp.float32),
            codes(hyps), codes(hyps), codes(2 * hyps), codes(2 * hyps), codes(hyps), codes(hyps),
            pltpu.VMEM((1, HEAD_DIM), jnp.int32),
            pltpu.VMEM((n, 1, HEAD_DIM), jnp.int32),
            pltpu.VMEM((n, ids, width), jnp.bfloat16),
            pltpu.VMEM((n, ids, width), jnp.bfloat16),
            pltpu.VMEM((chunks, hyps, rows, HEAD_DIM), jnp.float32),
            pltpu.VMEM((3, ids, HEAD_DIM), jnp.float32),
            pltpu.VMEM((2, chunks, rows, HEAD_DIM), jnp.float32),
            pltpu.VMEM((3, ids, HEAD_DIM), jnp.float32),
            pltpu.VMEM((SPLIT, rows, HEAD_DIM), jnp.float32),
            dma((3, chunks)), dma((3, chunks)), dma((n,)), dma((n,)), dma((n,)), dma((n,)),
            dma((heads,)), dma((chunks,)),
        ],
        compiler_params=pltpu.CompilerParams(collective_id=0, has_side_effects=True),
        name="step",
    )(
        states, next_token.reshape(1, hyps), parent_beam.reshape(1, hyps), proj_table,
        jnp.transpose(gate_table, (1, 2, 0)), gain,
    )


def solution(mesh):
    return jax.shard_map(
        local,
        mesh=mesh,
        in_specs=(
            P(("groups", "beam"), "mp", None, None),
            P(("groups", "beam")),
            P(("groups", "beam")),
            P("beam", "mp", None),
            P("beam", None, "mp"),
            P("mp", None),
        ),
        out_specs=(P(("groups", "beam"), "mp", None), P(("groups", "beam"), "mp", None, None)),
        check_vma=False,
    )
```

time: 53.2 us -> 49.9 us (0.938)
  Pallas kernels: 48.8 us -> 45.1 us
    pallas_call x1, Pallas kernels: 48.8 us -> 45.1 us  [local(): pl.pallas_call(lambda *refs: step_kernel(n, heads, hyps, vocab, *refs), o...]
where the time goes in v3:
time: 49.9 us; the launch traced here: 49.3 us
  Pallas kernels  45.1 us (90%)
  local copies, waits for them, and re-layouts  3.57 us (7%)
  between operations  0.64 us (1%)
    pallas_call x1, Pallas kernels, local(): pl.pallas_call(lambda *refs: step_kernel(n, heads, hyps, vocab, *refs), o...  45.1 us
    unnamed x2, local copies, waits for them, and re-layouts  3.57 us

profile of v3, /device:TPU:0, one launch (start us, length us, event | category | flops | bytes accessed | tf_op | source)
XLA Modules:
  0.0 49.3 jit_solution(7077650616858888505)
XLA Ops:
  0.6 45.1 %step.1 = (bf16[4,4,128]{2,1,0:T(4,128)(2,1)}, f32[4,4,128,128]{3,2,1,0:T(8,128)}) custom-call(f32[4,4,128,128]{3,2,1,0:T(8,128)} %refs_0_.1, s32[1,4]{1,0:T(1,128)} %bitcast.4, s32[1,4]{1,0:T(1,128)} %bitcast.5, bf16[128,4,640]{2,1,0:T(4,128)(2,1)} %refs_3_.1, bf16[3,4,128]{2,1,0:T(4,128)(2,1)} %bitcast.3, f32[4,128]{1,0:T(4,128)} %refs_5_.1), custom_call_target="tpu_custom_call" | custom-call | tf_op jit(solution)/shard_map/step/pallas_call | solution.py:272
  45.8 1.3 %copy.10 = bf16[4,4,128]{2,1,0:T(4,128)(2,1)} copy(bf16[4,4,128]{2,1,0:T(4,128)(2,1)} %get-tuple-element.4) | data formatting | bytes 8192
  47.0 2.3 %copy.11 = f32[4,4,128,128]{3,2,1,0:T(8,128)} copy(f32[4,4,128,128]{3,2,1,0:T(8,128)} %get-tuple-element.5) | data formatting | bytes 2097152

commit v4 on v3

--- a/solution.py
+++ b/solution.py
@@ -10,6 +10,7 @@
 SPLIT = 2
 AHEAD = 3
 LAG = 2
+LATE = 7
 PEAK = 4.0
 LEVELS = 32767.0
 MESH = pl.DeviceIdType.MESH
@@ -37,9 +38,9 @@
 
 
 def step_kernel(
-    n, heads, hyps, vocab, states, token, parent, table, gate, gain, readout, new_states,
+    n, heads, hyps, vocab, states, token, parent, table_home, gate, gain, readout, new_states,
     held, own, mir, xsnd, xrcv, zsnd, zrcv, mloc, mrcv, esnd, ercv, fresh,
-    keys, columns, strengths, outs,
+    keys, columns, strengths, outs, table, table_sem,
     send_sems, recv_sems, msend, mrecv, esend, erecv, load_sems, store_sems,
 ):
     me = lax.axis_index("beam")
@@ -96,6 +97,8 @@
 
     for h in range(heads):
         load(h).start()
+    table_load = pltpu.make_async_copy(table_home, table, table_sem)
+    table_load.start()
     barrier = pltpu.get_barrier_semaphore()
 
     def greet(j):
@@ -132,6 +135,7 @@
     head_of = lax.broadcasted_iota(jnp.int32, (ids, 1), 0) // hyps
     head_lane = lax.broadcasted_iota(jnp.int32, (ids, heads), 1) == head_of
     lane = lax.broadcasted_iota(jnp.int32, (ids, d), 1)
+    table_load.wait()
     flat = table[...].reshape(vocab * heads, 5 * d)
 
     def find(j):
@@ -146,10 +150,6 @@
             gates = jnp.where(lane == g, one, gates)
         esnd[j, :, 5 * d:6 * d] = gates.astype(jnp.bfloat16)
 
-        @pl.when(j > 0)
-        def _():
-            entry(j).start()
-
     repeat(0, n, find)
 
     place = lax.broadcasted_iota(jnp.int32, (1, d), 1)
@@ -199,6 +199,10 @@
                 xsnd[i, hyps + u] = jnp.where(at_diagonal[u] == beam, a, m).astype(jnp.int16)
             second(i).start()
 
+        @pl.when(i == chunks - AHEAD)
+        def _():
+            repeat(1, n, lambda j: entry(j).start())
+
         t = i - LAG
 
         @pl.when((t >= 0) & (t < chunks))
@@ -210,7 +214,7 @@
                 zsnd[t, u] = jnp.where(p == beam, a, jnp.where(p == across, m, x)).astype(jnp.int16)
             third(t).start()
 
-        f = i - 2 * LAG
+        f = i - LATE
 
         @pl.when(f == 0)
         def _():
@@ -236,7 +240,7 @@
                 outs[s] = jnp.where(out_lane == h * hyps + u, out, outs[s])
             store(f).start()
 
-    repeat(0, chunks + 2 * LAG, advance)
+    repeat(0, chunks + LATE, advance)
 
     out_rows = outs[...].reshape(d, d).T[0:ids]
     out_rows = out_rows * lax.rsqrt(jnp.mean(out_rows * out_rows, axis=-1, keepdims=True) + 1e-05)
@@ -253,6 +257,19 @@
         store(i).wait()
 
     repeat(0, chunks, finish)
+
+
+def place_kernel(hyps, rows_in, states_in, rows_out, states_out, held, loads, stores):
+    rows_out[...] = rows_in[...]
+    ins = [pltpu.make_async_copy(states_in.at[u], held.at[u], loads.at[u]) for u in range(hyps)]
+    outs = [pltpu.make_async_copy(held.at[u], states_out.at[u], stores.at[u]) for u in range(hyps)]
+    for c in ins:
+        c.start()
+    for u in range(hyps):
+        ins[u].wait()
+        outs[u].start()
+    for c in outs:
+        c.wait()
 
 
 def local(states, parent_beam, next_token, proj_table, gate_table, gain):
@@ -269,13 +286,13 @@
         return pltpu.VMEM((chunks, slots, rows, HEAD_DIM), jnp.int16)
 
     dma = pltpu.SemaphoreType.DMA
-    return pl.pallas_call(
+    result = pl.pallas_call(
         lambda *refs: step_kernel(n, heads, hyps, vocab, *refs),
         out_shape=(
             jax.ShapeDtypeStruct((hyps, heads, HEAD_DIM), jnp.bfloat16),
             jax.ShapeDtypeStruct(states.shape, jnp.float32),
         ),
-        in_specs=[hbm] + [vmem] * 5,
+        in_specs=[hbm, vmem, vmem, hbm, vmem, vmem],
         out_specs=(vmem, hbm),
         scratch_shapes=[
             pltpu.VMEM((heads, hyps, HEAD_DIM, HEAD_DIM), jnp.float32),
@@ -289,6 +306,8 @@
             pltpu.VMEM((2, chunks, rows, HEAD_DIM), jnp.float32),
             pltpu.VMEM((3, ids, HEAD_DIM), jnp.float32),
             pltpu.VMEM((SPLIT, rows, HEAD_DIM), jnp.float32),
+            pltpu.VMEM(proj_table.shape, proj_table.dtype),
+            dma,
             dma((3, chunks)), dma((3, chunks)), dma((n,)), dma((n,)), dma((n,)), dma((n,)),
             dma((heads,)), dma((chunks,)),
         ],
@@ -298,6 +317,14 @@
         states, next_token.reshape(1, hyps), parent_beam.reshape(1, hyps), proj_table,
         jnp.transpose(gate_table, (1, 2, 0)), gain,
     )
+    return pl.pallas_call(
+        lambda *refs: place_kernel(hyps, *refs),
+        out_shape=tuple(jax.ShapeDtypeStruct(r.shape, r.dtype) for r in result),
+        in_specs=[vmem, hbm],
+        out_specs=(vmem, hbm),
+        scratch_shapes=[pltpu.VMEM(states.shape, states.dtype), dma((hyps,)), dma((hyps,))],
+        name="place",
+    )(*result)
 
 
 def solution(mesh):

time: 49.9 us -> 48.3 us (0.968)
  local copies, waits for them, and re-layouts: 3.57 us -> 0 us
  Pallas kernels: 45.1 us -> 47.5 us
    unnamed x2 -> x0, local copies, waits for them, and re-layouts: 3.57 us -> none
    pallas_call x0 -> x1, Pallas kernels: none -> 3.25 us  [local(): pl.pallas_call(lambda *refs: place_kernel(hyps, *refs), out_shape=tuple((...]
    pallas_call x1, Pallas kernels: 45.1 us -> 44.2 us  [local(): pl.pallas_call(lambda *refs: step_kernel(n, heads, hyps, vocab, *refs), o...]
where the time goes in v4:
time: 48.3 us; the launch traced here: 48.1 us
  Pallas kernels  47.5 us (98%)
  between operations  0.64 us (1%)
    pallas_call x1, Pallas kernels, local(): pl.pallas_call(lambda *refs: step_kernel(n, heads, hyps, vocab, *refs), o...  44.2 us
    pallas_call x1, Pallas kernels, local(): pl.pallas_call(lambda *refs: place_kernel(hyps, *refs), out_shape=tuple((...  3.25 us

profile of v4, /device:TPU:0, one launch (start us, length us, event | category | flops | bytes accessed | tf_op | source)
XLA Modules:
  0.0 48.1 jit_solution(3012691357805026610)
XLA Ops:
  0.6 44.2 %step.1 = (bf16[4,4,128]{2,1,0:T(4,128)(2,1)}, f32[4,4,128,128]{3,2,1,0:T(8,128)}) custom-call(f32[4,4,128,128]{3,2,1,0:T(8,128)} %refs_0_.1, s32[1,4]{1,0:T(1,128)} %bitcast.4, s32[1,4]{1,0:T(1,128)} %bitcast.5, bf16[128,4,640]{2,1,0:T(4,128)(2,1)} %refs_3_.1, bf16[3,4,128]{2,1,0:T(4,128)(2,1)} %bitcast.3, f32[4,128]{1,0:T(4,128)} %refs_5_.1), custom_call_target="tpu_custom_call" | custom-call | tf_op jit(solution)/shard_map/step/pallas_call | solution.py:289
  44.9 3.2 %place.1 = (bf16[4,4,128]{2,1,0:T(4,128)(2,1)}, f32[4,4,128,128]{3,2,1,0:T(8,128)}) custom-call(bf16[4,4,128]{2,1,0:T(4,128)(2,1)} %get-tuple-element.4.refs_0_, f32[4,4,128,128]{3,2,1,0:T(8,128)} %get-tuple-element.5.refs_1_), custom_call_target="tpu_custom_call" | custom-call | tf_op jit(solution)/shard_map/place/pallas_call | solution.py:320
